TPU v7x, 32 devices: a whole 2x2x4 slice. The times are simulated.
32 devices in a mesh: group: 2 (over y), seq: 8 (over z, x), tensor: 2 (over core).
Axes of the slice: x: 2, y: 2, z: 4, core: 2. Of those that a mesh axis runs over, the one named last changes fastest.
Arguments:
- query: bfloat16 [32, 64, 128], P('group', 'tensor'), parts along dimension 0, may hold values from -400 to 400
- key_cache: bfloat16 [512, 128, 8, 128], P(('group', 'seq'), None, 'tensor'), parts along dimension 0, may hold values from -6 to 6
- value_cache: bfloat16 [512, 128, 8, 128], P(('group', 'seq'), None, 'tensor'), parts along dimension 0, may hold values from -6 to 6
- lengths: int32 [32], P('group'), parts along dimension 0, may hold values from 1 to 8192, 14336 in all
- page_order: int32 [512], P('group'), parts along dimension 0, may hold values from 0 to 255, as said below
- out_weight: bfloat16 [8192, 8192], P('tensor', 'seq'), may hold values from -0.59765625 to 0.59765625
Outputs:
- mixed: bfloat16 [32, 8192], P(('group', 'tensor'), 'seq'), parts along dimension 0
There are 2 independent parts, one for each index of `group`. A program takes and returns all parts, laid end to end along the dimension named above; an argument that names none is the same for every part. Nothing has to cross between parts.
Inputs may be any that keep to these rules, and one draw needn't show every extreme that they name: The sequences' lengths sum to 14336; one equals 8192. `page_order`: a permutation of the pages.
All inputs are finite; a program needn't handle non-finite values.
Results may differ from a plain program's by a relative error of at most 0.0065.
Values may be sent and summed in bfloat16 or wider, within the bound.
A program may use at most 64 MiB of HBM per device.

v0:
```python
import math

import jax
import jax.numpy as jnp
from jax import lax
from jax.sharding import PartitionSpec as P


def merged(value, axis, combine):
    everything = jax.tree.map(lambda part: lax.all_gather(part, axis), value)
    initial = jax.tree.map(lambda part: part[0], everything)

    def lap(k, so_far):
        return combine(so_far, jax.tree.map(lambda part: part[k], everything))

    return lax.fori_loop(1, lax.axis_size(axis), lap, initial)


def combine_parts(first_part, second_part):
    first_max, first_sum, first_out = first_part
    second_max, second_sum, second_out = second_part
    head_dim = first_out.shape[1] // first_max.shape[1]
    largest = jnp.maximum(first_max, second_max)
    first_factor = jnp.exp(first_max - largest)
    second_factor = jnp.exp(second_max - largest)
    merged_sum = first_sum * first_factor + second_sum * second_factor
    merged_out = first_out * jnp.repeat(first_factor, head_dim, axis=1) + second_out * jnp.repeat(
        second_factor, head_dim, axis=1
    )
    return (largest, merged_sum, merged_out)


def body(query, key_cache, value_cache, lengths, page_order, out_weight):
    pages_dev, page_len, kv_local, head_dim = key_cache.shape
    seq_count, heads_local = (query.shape[0], query.shape[1])
    group_size = heads_local // kv_local
    pool_size = page_order.shape[0]
    score_scale = 1.0 / math.sqrt(head_dim)
    counts = (lengths + page_len - 1) // page_len
    starts = jnp.cumsum(counts) - counts
    used_total = jnp.sum(counts)
    page_rank = (
        jnp.zeros((pool_size,), jnp.int32)
        .at[page_order]
        .set(jnp.arange(pool_size, dtype=jnp.int32))
    )
    first_page = lax.axis_index("seq") * pages_dev
    local_rank = lax.dynamic_slice_in_dim(page_rank, first_page, pages_dev)
    is_live = local_rank < used_total
    page_owner = jnp.sum((local_rank[:, None] >= starts[None, :]).astype(jnp.int32), axis=1) - 1
    page_owner = jnp.where(is_live, page_owner, -1)
    owner_safe = jnp.clip(page_owner, 0, seq_count - 1)
    block_index = local_rank - starts[owner_safe]
    positions = block_index[:, None] * page_len + jnp.arange(page_len, dtype=jnp.int32)[None, :]
    is_valid = is_live[:, None] & (positions < lengths[owner_safe][:, None])
    page_query = query[owner_safe].reshape(pages_dev, kv_local, group_size, head_dim)
    scores = (
        jnp.einsum("pghd,ptgd->pght", page_query, key_cache, preferred_element_type=jnp.float32)
        * score_scale
    )
    score_mask = is_valid[:, None, None, :]
    scores = jnp.where(score_mask, scores, -1e30)
    block_max = jnp.max(scores, axis=-1)
    weights = jnp.where(score_mask, jnp.exp(scores - block_max[..., None]), 0.0).astype(
        jnp.bfloat16
    )
    block_sum = jnp.sum(weights.astype(jnp.float32), axis=-1)
    block_out = jnp.einsum(
        "pght,ptgd->pghd", weights, value_cache, preferred_element_type=jnp.float32
    )
    flat_max = block_max.reshape(pages_dev, heads_local)
    onehot = page_owner[None, :] == jnp.arange(seq_count, dtype=jnp.int32)[:, None]
    seq_max = jnp.max(jnp.where(onehot[:, :, None], flat_max[None], -1e30), axis=1)
    factor = jnp.exp(flat_max - seq_max[owner_safe])
    onehot_wide = onehot.astype(jnp.float32)
    seq_sum = jnp.dot(
        onehot_wide,
        factor * block_sum.reshape(pages_dev, heads_local),
        precision=lax.Precision.HIGHEST,
    )
    scaled_out = (factor[:, :, None] * block_out.reshape(pages_dev, heads_local, head_dim)).reshape(
        pages_dev, heads_local * head_dim
    )
    seq_out = jnp.dot(onehot_wide, scaled_out, precision=lax.Precision.HIGHEST)
    largest, denominator, numerator = merged((seq_max, seq_sum, seq_out), "seq", combine_parts)
    attended = (numerator / jnp.repeat(denominator, head_dim, axis=1)).astype(jnp.bfloat16)
    projected = jnp.dot(attended, out_weight, preferred_element_type=jnp.float32)
    return lax.psum_scatter(projected, "tensor", scatter_dimension=0, tiled=True).astype(
        jnp.bfloat16
    )


def solution(mesh):
    in_specs = (
        P("group", "tensor", None),
        P(("group", "seq"), None, "tensor", None),
        P(("group", "seq"), None, "tensor", None),
        P("group"),
        P("group"),
        P("tensor", "seq"),
    )
    out_specs = P(("group", "tensor"), "seq")
    return jax.shard_map(body, mesh=mesh, in_specs=in_specs, out_specs=out_specs, check_vma=False)
```

profile of v0, /device:TPU:0, one launch (start us, length us, event | category | flops | bytes accessed | tf_op | source)
XLA Modules:
  0.0 123.4 jit_solution(17163994939558254719)
XLA Ops:
  6.5 0.7 compare_select_fusion
  7.3 1.3 %fusion.30 = (s32[]{:T(128)}, s32[16]{0:T(128)S(1)}) fusion(s32[16]{0:T(128)} %param.11), kind=kLoop, calls=%fused_computation.54 | loop fusion | flops 271 | bytes 132 | tf_op jit(solution)/shard_map/reduce_sum | solution.py:41
  8.8 1.4 %scatter_custom_fusion = s32[256]{0:T(256)S(1)} fusion(s32[256]{0:T(256)S(1)} %compare_select_fusion, s32[256]{0:T(256)S(1)} %iota.19, s32[]{:T(128)} %constant.74.clone.1), kind=kCustom, calls=%fused_computation.50 | custom fusion | bytes 1028 | tf_op jit(solution)/shard_map/scatter | solution.py:45
  10.4 0.7 compare_select_fusion.1
  11.1 0.7 gather_fusion
  11.8 1.4 %gather_fusion.1 = s32[32]{0:T(128)S(1)} fusion(s32[16]{0:T(128)} %param.11, s32[1024]{0:T(1024)S(1)} %pad_clamp_fusion), kind=kCustom, calls=%fused_computation.1 | custom fusion | bytes 384 | tf_op jit(solution)/shard_map/gather | solution.py:55
  13.3 0.6 gather_fusion.2
  14.0 4.6 %fusion.31 = (f32[32,4,8]{2,1,0:T(4,128)S(1)}, f32[32,4,8,128]{3,2,1,0:T(8,128)S(1)}) fusion(bf16[32,128,4,128]{3,2,1,0:T(4,128)(2,1)} %param.9, bf16[32,32,128]{2,1,0:T(8,128)(2,1)S(1)} %gather_fusion.2, pred[32,128]{1,0:T(8,128)(4,1)S(1)} %fusion.23), kind=kOutput, calls=%fused_computation.55 | convolution fusion | flops 33946624 | bytes 4988928 | tf_op jit(solution)/shard_map/pghd,ptgd->pght/dot_general | solution.py:58
  18.7 0.2 select_reduce_fusion
  18.8 0.6 gather_fusion.3
  19.4 3.4 %fusion.3 = f32[32,4,8,128]{3,2,1,0:T(8,128)S(1)} fusion(bf16[32,128,4,128]{3,2,1,0:T(4,128)(2,1)} %param.10, f32[32,4,8,128]{3,2,1,0:T(8,128)S(1)} %get-tuple-element.208, f32[32,4,8]{2,1,0:T(4,128)S(1)} %get-tuple-element.207, pred[32,128]{1,0:T(8,128)(4,1)S(1)} %fusion.23), kind=kOutput, calls=%fused_computation.14 | convolution fusion | flops 33947648 | bytes 5251072 | tf_op jit(solution)/shard_map/pght,ptgd->pghd/dot_general | solution.py:68
  22.9 0.2 mul.76
  23.1 1.7 %fusion.13 = f32[16,4096]{1,0:T(8,128)} fusion(f32[4,8,32,128]{3,2,1,0:T(8,128)S(1)} %bitcast.67, f32[4,8,32,128]{3,2,1,0:T(8,128)S(1)} %bitcast.68, s32[32]{0:T(128)S(1)} %get-tuple-element.203), kind=kOutput, calls=%fused_computation.21 | convolution fusion | flops 25297408 | bytes 1310848 | tf_op jit(solution)/shard_map/dot_general | solution.py:84
  24.9 32.5 %all-gather = f32[128,32]{1,0:T(8,128)S(1)} all-gather(f32[16,32]{1,0:T(8,128)S(1)} %select_reduce_fusion), channel_id=2, replica_groups=mesh['group'=2,'seq'=8,'tensor'=2] {'seq'}, dimensions={0}, use_global_device_ids=true | all-gather | bytes 18432 | tf_op jit(solution)/shard_map/all_gather | solution.py:10
  57.4 0.4 convert_reduce_fusion
  58.0 0.1 fusion.21
  58.1 30.9 %all-gather.1 = f32[128,32]{1,0:T(8,128)S(1)} all-gather(f32[16,32]{1,0:T(8,128)S(1)} %fusion.21), channel_id=3, replica_groups=mesh['group'=2,'seq'=8,'tensor'=2] {'seq'}, dimensions={0}, use_global_device_ids=true | all-gather | bytes 18432 | tf_op jit(solution)/shard_map/all_gather | solution.py:10
  89.0 1.0 slice.25
  90.0 11.2 %while.19 = (s32[]{:T(128)}, f32[16,32]{1,0:T(8,128)S(1)}, f32[16,32]{1,0:T(8,128)S(1)}, f32[16,4096]{1,0:T(8,128)S(1)}, f32[8,16,32]{2,1,0:T(8,128)S(1)}, /*ind...) while((s32[]{:T(128)}, f32[16,32]{1,0:T(8,128)S(1)}, ...), condition=%wide.region_8.9_spmd, body=%wide.region_7.8_spmd.sunk | while | flops 199685 | bytes 1855631 | solution.py:16
  90.3 1.3 %fusion.36 = f32[16,4096]{1,0:T(8,128)S(1)} fusion(f32[2,8,32,128]{3,2,1,0:T(8,128)S(1)} %bitcast.65, f32[16,4096]{1,0:T(8,128)S(1)} %get-tuple-element.273, f32[2,8,32,128]{3,2,1,0:T(8,128)S(1)} %bitcast.66, f32[8,16,4096]{2,1,0:T(8,128)} %get-tuple-element.286, s32[]{:T(128)S(6)} %select_n.65), kind=kLoop, calls=%fused_computation.6.clone.1 | loop fusion | flops 196608 | bytes 1310724 | tf_op jit(solution)/shard_map/while/body/eval_jaxpr/add | solution.py:27
  91.9 1.3 %fusion.36 = f32[16,4096]{1,0:T(8,128)S(1)} fusion(f32[2,8,32,128]{3,2,1,0:T(8,128)S(1)} %bitcast.65, f32[16,4096]{1,0:T(8,128)S(1)} %get-tuple-element.273, f32[2,8,32,128]{3,2,1,0:T(8,128)S(1)} %bitcast.66, f32[8,16,4096]{2,1,0:T(8,128)} %get-tuple-element.286, s32[]{:T(128)S(6)} %select_n.65), kind=kLoop, calls=%fused_computation.6.clone.1 | loop fusion | flops 196608 | bytes 1310724 | tf_op jit(solution)/shard_map/while/body/eval_jaxpr/add | solution.py:27
  93.5 1.3 %fusion.36 = f32[16,4096]{1,0:T(8,128)S(1)} fusion(f32[2,8,32,128]{3,2,1,0:T(8,128)S(1)} %bitcast.65, f32[16,4096]{1,0:T(8,128)S(1)} %get-tuple-element.273, f32[2,8,32,128]{3,2,1,0:T(8,128)S(1)} %bitcast.66, f32[8,16,4096]{2,1,0:T(8,128)} %get-tuple-element.286, s32[]{:T(128)S(6)} %select_n.65), kind=kLoop, calls=%fused_computation.6.clone.1 | loop fusion | flops 196608 | bytes 1310724 | tf_op jit(solution)/shard_map/while/body/eval_jaxpr/add | solution.py:27
  94.8 0.1 broadcast_in_dim.111
  95.1 1.3 %fusion.36 = f32[16,4096]{1,0:T(8,128)S(1)} fusion(f32[2,8,32,128]{3,2,1,0:T(8,128)S(1)} %bitcast.65, f32[16,4096]{1,0:T(8,128)S(1)} %get-tuple-element.273, f32[2,8,32,128]{3,2,1,0:T(8,128)S(1)} %bitcast.66, f32[8,16,4096]{2,1,0:T(8,128)} %get-tuple-element.286, s32[]{:T(128)S(6)} %select_n.65), kind=kLoop, calls=%fused_computation.6.clone.1 | loop fusion | flops 196608 | bytes 1310724 | tf_op jit(solution)/shard_map/while/body/eval_jaxpr/add | solution.py:27
  96.4 0.1 broadcast_in_dim.111
  96.7 1.3 %fusion.36 = f32[16,4096]{1,0:T(8,128)S(1)} fusion(f32[2,8,32,128]{3,2,1,0:T(8,128)S(1)} %bitcast.65, f32[16,4096]{1,0:T(8,128)S(1)} %get-tuple-element.273, f32[2,8,32,128]{3,2,1,0:T(8,128)S(1)} %bitcast.66, f32[8,16,4096]{2,1,0:T(8,128)} %get-tuple-element.286, s32[]{:T(128)S(6)} %select_n.65), kind=kLoop, calls=%fused_computation.6.clone.1 | loop fusion | flops 196608 | bytes 1310724 | tf_op jit(solution)/shard_map/while/body/eval_jaxpr/add | solution.py:27
  98.3 1.3 %fusion.36 = f32[16,4096]{1,0:T(8,128)S(1)} fusion(f32[2,8,32,128]{3,2,1,0:T(8,128)S(1)} %bitcast.65, f32[16,4096]{1,0:T(8,128)S(1)} %get-tuple-element.273, f32[2,8,32,128]{3,2,1,0:T(8,128)S(1)} %bitcast.66, f32[8,16,4096]{2,1,0:T(8,128)} %get-tuple-element.286, s32[]{:T(128)S(6)} %select_n.65), kind=kLoop, calls=%fused_computation.6.clone.1 | loop fusion | flops 196608 | bytes 1310724 | tf_op jit(solution)/shard_map/while/body/eval_jaxpr/add | solution.py:27
  99.6 0.1 broadcast_in_dim.111
  99.9 1.3 %fusion.36 = f32[16,4096]{1,0:T(8,128)S(1)} fusion(f32[2,8,32,128]{3,2,1,0:T(8,128)S(1)} %bitcast.65, f32[16,4096]{1,0:T(8,128)S(1)} %get-tuple-element.273, f32[2,8,32,128]{3,2,1,0:T(8,128)S(1)} %bitcast.66, f32[8,16,4096]{2,1,0:T(8,128)} %get-tuple-element.286, s32[]{:T(128)S(6)} %select_n.65), kind=kLoop, calls=%fused_computation.6.clone.1 | loop fusion | flops 196608 | bytes 1310724 | tf_op jit(solution)/shard_map/while/body/eval_jaxpr/add | solution.py:27
  101.3 5.3 %fusion.19 = f32[16,1024]{1,0:T(8,128)} fusion(bf16[4096,1024]{1,0:T(8,128)(2,1)} %param.13, f32[16,4096]{1,0:T(8,128)S(1)} %get-tuple-element.182, f32[2,8,32,128]{3,2,1,0:T(8,128)S(1)} %bitcast.70), kind=kOutput, calls=%fused_computation.31 | convolution fusion | flops 134348800 | bytes 8978432 | tf_op jit(solution)/shard_map/dot_general | solution.py:87
  106.6 8.6 %reduce-scatter.2.cloned.1.call-done = f32[8,1024]{1,0:T(8,128)} async-done(((f32[16,1024]{1,0:T(8,128)}), f32[8,1024]{1,0:T(8,128)}) %reduce-scatter.2.cloned.1.call-update) | async-done | bytes 32784 | tf_op jit(solution)/shard_map/reduce_scatter | solution.py:88
  115.2 1.4 %convert_element_type.20 = bf16[8,1024]{1,0:T(8,128)(2,1)} convert(f32[8,1024]{1,0:T(8,128)} %reduce-scatter.2.cloned.1.call-done) | non-fusion elementwise | flops 8192 | bytes 49152 | tf_op jit(solution)/shard_map/convert_element_type | solution.py:88
  (44 shorter events, 2.6 us)
Async XLA Ops:
  6.5 6.7 %copy-start = (bf16[16,32,128]{2,1,0:T(8,128)(2,1)S(1)}, bf16[16,32,128]{2,1,0:T(8,128)(2,1)}, u32[]{:S(2)}) copy-start(bf16[16,32,128]{2,1,0:T(8,128)(2,1)} %param.8) | copy-start | bytes 393220
  6.5 82.5 %all-gather.5.cloned.1.call-start = ((), (), s32[]{:S(2)}) async-start(), calls=%async_computation.2 | async-start | bytes 2359296 | tf_op jit(solution)/shard_map/all_gather | solution.py:10
  24.8 90.4 %reduce-scatter.2.cloned.1.call-start = ((), (), s32[]{:S(2)}) async-start(), calls=%async_computation.1 | async-start | bytes 98304 | tf_op jit(solution)/shard_map/reduce_scatter | solution.py:88
Sparse Core Ops, SparseCore 0:
  24.9 52.6 all-gather.4
  106.7 8.4 reduce-scatter.1
where the time goes:
time: 124 us; the launch traced here: 123 us
  blocking collectives  63.4 us (51%)
  matrix products  15.1 us (12%)
  other arithmetic  14.3 us (12%)
  between operations  13.5 us (11%)
  waiting for transfers between devices  8.65 us (7%)
  local copies, waits for them, and re-layouts  8.16 us (7%)
    all_gather x2, blocking collectives, merged(): everything = jax.tree.map(lambda part: lax.all_gather(part, axis), value)  63.4 us
    add x7, other arithmetic, combine_parts(): first_out * jnp.repeat(first_factor, head_dim, axis=1)  9.02 us
    reduce_scatter x1, waiting for transfers between devices, body(): lax.psum_scatter(projected, 'tensor', scatter_dimension=0, tiled=True)  8.62 us
    dot_general x1, matrix products, body(): jnp.dot(attended, out_weight, preferred_element_type=jnp.float32)  5.25 us
    dot_general x1, matrix products, body(): jnp.einsum('pghd,ptgd->pght', page_query, key_cache, preferred_element_ty...  4.57 us
    dot_general x1, matrix products, body(): jnp.einsum('pght,ptgd->pghd', weights, value_cache, preferred_element_typ...  3.44 us
  transfers between devices with their start and end apart: 2, of which 1 were waited for; matrix products, arithmetic and copies ran while one was open for 1% of the time, Pallas kernels for 0%

commit v1 on v0

v1 whole, which is shorter than its diff:
```python
import functools
import math

import jax
import jax.numpy as jnp
from jax import lax
from jax.experimental import pallas as pl
from jax.experimental.pallas import tpu as pltpu
from jax.sharding import PartitionSpec as P

MASKED = -1e30
FLOOR = -1e29
LANES = 128
MESH = pl.DeviceIdType.MESH


def attend_kernel(
    page_len,
    group_size,
    chunk,
    exponent_scale,
    lengths_ref,
    order_ref,
    query_ref,
    key_hbm,
    value_hbm,
    out_ref,
    stats_ref,
    keys,
    values,
    scores,
    meta_vector,
    meta,
    top,
    total,
    gathered,
    by_head,
    key_sems,
    value_sems,
    meta_sem,
):
    pages, rows, head_dim = keys.shape
    seqs, heads, _ = query_ref.shape
    kv_local = rows // page_len
    shards, shard_rows, _ = out_ref.shape
    chunks = pages // chunk

    def key_copy(c):
        part = pl.ds(c * chunk, chunk)
        return pltpu.make_async_copy(key_hbm.at[part], keys.at[part], key_sems.at[c])

    def value_copy(c):
        part = pl.ds(c * chunk, chunk)
        return pltpu.make_async_copy(value_hbm.at[part], values.at[part], value_sems.at[c])

    for c in range(chunks):
        key_copy(c).start()
    for c in range(chunks):
        value_copy(c).start()

    pool = order_ref.shape[0]
    order = order_ref[...].reshape(1, pool)
    rank = lax.broadcasted_iota(jnp.int32, (1, pool), 1)
    owner_row = jnp.zeros((1, pool), jnp.int32)
    limit_row = jnp.zeros((1, pool), jnp.int32)
    start = jnp.int32(0)
    for s in range(seqs):
        length = lengths_ref[s]
        reached = rank >= start
        owner_row = jnp.where(reached, s, owner_row)
        limit_row = jnp.where(reached, length + start * page_len, limit_row)
        start = start + lax.div(length + (page_len - 1), page_len)
    valid_row = jnp.clip(limit_row - rank * page_len, 0, page_len)
    packed = (owner_row * (2 * page_len) + valid_row).astype(jnp.float32)
    local_page = lax.axis_index("seq") * pages + lax.broadcasted_iota(jnp.int32, (pages, pool), 0)
    found = jnp.sum(jnp.where(order == local_page, packed, 0.0), axis=1, keepdims=True)
    meta_vector[...] = jnp.broadcast_to(found, (pages, LANES)).astype(jnp.int32)
    meta_copy = pltpu.make_async_copy(meta_vector, meta, meta_sem)
    meta_copy.start()

    top[...] = jnp.full(top.shape, FLOOR, jnp.float32)
    total[...] = jnp.zeros(total.shape, jnp.float32)
    gathered[...] = jnp.zeros(gathered.shape, jnp.float32)
    column = lax.broadcasted_iota(jnp.int32, (heads, rows), 1)
    row_head = lax.broadcasted_iota(jnp.int32, (heads, rows), 0) // group_size
    column_limit = jnp.where(column % kv_local == row_head, column, rows)
    meta_copy.wait()

    def owner_of(p):
        return lax.div(meta[p, 0], 2 * page_len)

    @pl.loop(0, chunks)
    def _(c):
        key_copy(c).wait()
        for i in range(chunk):
            p = c * chunk + i
            owner = owner_of(p)
            count = lax.rem(meta[p, 0], 2 * page_len) * kv_local
            score = lax.dot_general(
                query_ref[owner],
                keys[p],
                (((1,), (1,)), ((), ())),
                preferred_element_type=jnp.float32,
            )
            score = jnp.where(column_limit < count, score, MASKED)
            scores[p] = score
            block_max = jnp.max(score, axis=1, keepdims=True)
            top[owner] = jnp.maximum(top[owner], jnp.broadcast_to(block_max, (heads, LANES)))

    @pl.loop(0, chunks)
    def _(c):
        value_copy(c).wait()
        for i in range(chunk):
            p = c * chunk + i
            owner = owner_of(p)
            highest = jnp.concatenate([top[owner]] * (rows // LANES), axis=1)
            weight = jnp.exp2((scores[p] - highest) * exponent_scale).astype(jnp.bfloat16)
            wide = weight.astype(jnp.float32)
            partial = wide[:, :LANES]
            for b in range(1, rows // LANES):
                partial = partial + wide[:, b * LANES : (b + 1) * LANES]
            total[owner] = total[owner] + partial
            gathered[owner] = gathered[owner] + jnp.dot(
                weight, values[p], preferred_element_type=jnp.float32
            )

    for s in range(seqs):
        where = pl.ds(s, heads, stride=seqs)
        by_head[0, where, :] = gathered[s]
        by_head[1, where, :] = top[s]
        by_head[2, where, :] = jnp.broadcast_to(
            jnp.sum(total[s], axis=1, keepdims=True), (heads, LANES)
        )
    out_ref[...] = by_head[0].reshape(shards, shard_rows, head_dim).astype(out_ref.dtype)
    diagonal = lax.broadcasted_iota(jnp.int32, (shard_rows, LANES), 0) == (
        lax.broadcasted_iota(jnp.int32, (shard_rows, LANES), 1)
    )
    for j in range(shards):
        for k in range(2):
            part = by_head[1 + k, j * shard_rows : (j + 1) * shard_rows, :]
            stats_ref[j, k : k + 1, :] = jnp.sum(
                jnp.where(diagonal, part, 0.0), axis=0, keepdims=True
            )


def mix_kernel(
    seqs,
    exponent_scale,
    partial_ref,
    stats_ref,
    weight_hbm,
    out_ref,
    outs_in,
    stats_in,
    attended,
    weight,
    sums,
    sums_in,
    weight_sems,
    out_send,
    out_recv,
    stats_send,
    stats_recv,
    att_send,
    att_recv,
    sum_send,
    sum_recv,
):
    shards, shard_rows, head_dim = partial_ref.shape
    ways = sums.shape[0]
    me = lax.axis_index("seq")
    half = lax.axis_index("tensor")
    pieces = weight_sems.shape[0]
    depth = weight.shape[0] // pieces
    loads = []
    for c in range(pieces):
        part = pl.ds(c * depth, depth)
        loads.append(
            pltpu.make_async_copy(weight_hbm.at[part], weight.at[part], weight_sems.at[c])
        )

    barrier = pltpu.get_barrier_semaphore()
    for k in range(1, shards):
        pl.semaphore_signal(
            barrier, inc=1, device_id={"seq": lax.rem(me + k, shards)}, device_id_type=MESH
        )
    for k in range(1, ways):
        pl.semaphore_signal(
            barrier, inc=1, device_id={"tensor": lax.rem(half + k, ways)}, device_id_type=MESH
        )
    for load in loads:
        load.start()
    pl.semaphore_wait(barrier, shards + ways - 2)

    sends = []
    for k in range(1, shards):
        peer = lax.rem(me + k, shards)
        for source, target, send, recv in (
            (stats_ref, stats_in, stats_send, stats_recv),
            (partial_ref, outs_in, out_send, out_recv),
        ):
            copy = pltpu.make_async_remote_copy(
                src_ref=source.at[peer],
                dst_ref=target.at[k],
                send_sem=send.at[k],
                recv_sem=recv.at[k],
                device_id={"seq": peer},
                device_id_type=MESH,
            )
            copy.start()
            sends.append(copy)
    stats_in[0] = stats_ref[me]
    for copy in sends[0::2]:
        copy.wait_recv()
    tops = jnp.concatenate([stats_in[k, 0:1, :] for k in range(shards)], axis=0)
    totals = jnp.concatenate([stats_in[k, 1:2, :] for k in range(shards)], axis=0)
    factor = jnp.exp2((tops - jnp.max(tops, axis=0, keepdims=True)) * exponent_scale)
    denominator = jnp.sum(factor * totals, axis=0, keepdims=True)
    used = lax.broadcasted_iota(jnp.int32, (1, LANES), 1) < shard_rows
    share = factor / jnp.where(used, denominator, 1.0)
    diagonal = lax.broadcasted_iota(jnp.int32, (shard_rows, LANES), 0) == (
        lax.broadcasted_iota(jnp.int32, (shard_rows, LANES), 1)
    )

    def column(k):
        return jnp.sum(jnp.where(diagonal, share[k : k + 1, :], 0.0), axis=1, keepdims=True)

    columns = [column(k) for k in range(shards)]
    mine = columns[0] * partial_ref[me].astype(jnp.float32)
    for k in range(1, shards):
        sends[2 * k - 1].wait_recv()
        mine = mine + columns[k] * outs_in[k].astype(jnp.float32)
    attended[me] = mine.astype(jnp.bfloat16)

    gathers = []
    for k in range(1, shards):
        copy = pltpu.make_async_remote_copy(
            src_ref=attended.at[me],
            dst_ref=attended.at[me],
            send_sem=att_send.at[k],
            recv_sem=att_recv.at[k],
            device_id={"seq": lax.rem(me + k, shards)},
            device_id_type=MESH,
        )
        copy.start()
        gathers.append(copy)
    for load in loads:
        load.wait()

    whole_heads = shard_rows // seqs
    if shard_rows % seqs == 0:
        span = whole_heads * head_dim
        result = None
        for k in range(shards):
            source = lax.rem(me + shards - k, shards)
            if k:
                pltpu.make_async_remote_copy(
                    src_ref=attended.at[source],
                    dst_ref=attended.at[source],
                    send_sem=att_send.at[k],
                    recv_sem=att_recv.at[k],
                    device_id={"seq": lax.rem(me + k, shards)},
                    device_id_type=MESH,
                ).wait_recv()
            block = attended[source]
            left = jnp.concatenate(
                [block[h * seqs : (h + 1) * seqs] for h in range(whole_heads)], axis=1
            )
            rows = weight[pl.ds(pl.multiple_of(source * span, span), span), :]
            product = jnp.dot(left, rows, preferred_element_type=jnp.float32)
            result = product if result is None else result + product
    else:
        for k in range(1, shards):
            gathers[k - 1].wait_recv()
        per_head = seqs // shard_rows
        result = None
        for h in range(shards // per_head):
            left = jnp.concatenate(
                [attended[h * per_head + i].astype(jnp.float32) for i in range(per_head)], axis=0
            ).astype(jnp.bfloat16)
            product = jnp.dot(
                left,
                weight[h * head_dim : (h + 1) * head_dim, :],
                preferred_element_type=jnp.float32,
            )
            result = product if result is None else result + product

    kept = seqs // ways
    for i in range(ways):
        sums[i] = result[i * kept : (i + 1) * kept]
    shares = []
    for k in range(1, ways):
        peer = lax.rem(half + k, ways)
        copy = pltpu.make_async_remote_copy(
            src_ref=sums.at[peer],
            dst_ref=sums_in.at[k - 1],
            send_sem=sum_send.at[k],
            recv_sem=sum_recv.at[k],
            device_id={"tensor": peer},
            device_id_type=MESH,
        )
        copy.start()
        shares.append(copy)
    mixed = sums[half]
    for k in range(1, ways):
        shares[k - 1].wait_recv()
        mixed = mixed + sums_in[k - 1]
    out_ref[...] = mixed.astype(out_ref.dtype)
    for copy in sends + gathers + shares:
        copy.wait_send()


def body(shards, ways, query, key_cache, value_cache, lengths, page_order, out_weight):
    pages, page_len, kv_local, head_dim = key_cache.shape
    seqs, heads, _ = query.shape
    rows = page_len * kv_local
    shard_rows = seqs * heads // shards
    chunk = 4
    exponent_scale = math.log2(math.e) / math.sqrt(head_dim)
    vmem = pl.BlockSpec(memory_space=pltpu.VMEM)
    smem = pl.BlockSpec(memory_space=pltpu.SMEM)
    hbm = pl.BlockSpec(memory_space=pl.ANY)
    f32, bf16 = jnp.float32, jnp.bfloat16
    dma = pltpu.SemaphoreType.DMA

    partial, stats = pl.pallas_call(
        functools.partial(attend_kernel, page_len, heads // kv_local, chunk, exponent_scale),
        out_shape=(
            jax.ShapeDtypeStruct((shards, shard_rows, head_dim), bf16),
            jax.ShapeDtypeStruct((shards, 2, LANES), f32),
        ),
        in_specs=[smem, vmem, vmem, hbm, hbm],
        out_specs=(vmem, vmem),
        scratch_shapes=[
            pltpu.VMEM((pages, rows, head_dim), bf16),
            pltpu.VMEM((pages, rows, head_dim), bf16),
            pltpu.VMEM((pages, heads, rows), f32),
            pltpu.VMEM((pages, LANES), jnp.int32),
            pltpu.SMEM((pages, LANES), jnp.int32),
            pltpu.VMEM((seqs, heads, LANES), f32),
            pltpu.VMEM((seqs, heads, LANES), f32),
            pltpu.VMEM((seqs, heads, head_dim), f32),
            pltpu.VMEM((3, seqs * heads, LANES), f32),
            dma((pages // chunk,)),
            dma((pages // chunk,)),
            dma,
        ],
    )(
        lengths,
        page_order,
        query,
        key_cache.reshape(pages, rows, head_dim),
        value_cache.reshape(pages, rows, head_dim),
    )

    depth, width = out_weight.shape
    kept = seqs // ways
    return pl.pallas_call(
        functools.partial(mix_kernel, seqs, exponent_scale),
        out_shape=jax.ShapeDtypeStruct((kept, width), bf16),
        in_specs=[vmem, vmem, hbm],
        out_specs=vmem,
        scratch_shapes=[
            pltpu.VMEM((shards, shard_rows, head_dim), bf16),
            pltpu.VMEM((shards, 2, LANES), f32),
            pltpu.VMEM((shards, shard_rows, head_dim), bf16),
            pltpu.VMEM((depth, width), bf16),
            pltpu.VMEM((ways, kept, width), f32),
            pltpu.VMEM((max(ways - 1, 1), kept, width), f32),
            dma((8,)),
            dma((shards,)),
            dma((shards,)),
            dma((shards,)),
            dma((shards,)),
            dma((shards,)),
            dma((shards,)),
            dma((ways,)),
            dma((ways,)),
        ],
        compiler_params=pltpu.CompilerParams(collective_id=0, has_side_effects=True),
    )(partial, stats, out_weight)


def solution(mesh):
    in_specs = (
        P("group", "tensor", None),
        P(("group", "seq"), None, "tensor", None),
        P(("group", "seq"), None, "tensor", None),
        P("group"),
        P("group"),
        P("tensor", "seq"),
    )
    out_specs = P(("group", "tensor"), "seq")
    step = functools.partial(body, mesh.shape["seq"], mesh.shape["tensor"])
    return jax.shard_map(step, mesh=mesh, in_specs=in_specs, out_specs=out_specs, check_vma=False)
```

time: 124 us -> 28.8 us (0.23)
  blocking collectives: 63.4 us -> 0 us
  Pallas kernels: 0 us -> 27.2 us
  matrix products: 15.1 us -> 0 us
  other arithmetic: 14.3 us -> 0 us
  between operations: 13.5 us -> 0.02 us
  waiting for transfers between devices: 8.65 us -> 0 us
  local copies, waits for them, and re-layouts: 8.16 us -> 1.32 us
    all_gather x2 -> x0, blocking collectives: 63.4 us -> none  [merged(): everything = jax.tree.map(lambda part: lax.all_gather(part, axis), value)]
    pallas_call x0 -> x2, Pallas kernels: none -> 27.2 us  [the longest x1 19.5 us: body(): pl.pallas_call(functools.partial(mix_kernel, seqs, exponent_scale), out_s...]
    dot_general x5 -> x0, matrix products: 15.1 us -> none  [the longest x1 5.25 us: body(): jnp.dot(attended, out_weight, preferred_element_type=jnp.float32)]
    add x14 -> x0, other arithmetic: 9.15 us -> none  [the longest x7 9.02 us: combine_parts(): first_out * jnp.repeat(first_factor, head_dim, axis=1)]
    reduce_scatter x1 -> x0, waiting for transfers between devices: 8.62 us -> none  [body(): lax.psum_scatter(projected, 'tensor', scatter_dimension=0, tiled=True)]
    gather x4 -> x0, local copies, waits for them, and re-layouts: 3.23 us -> none  [the longest x1 1.36 us: body(): is_valid = is_live[:, None] & (positions < lengths[owner_safe][:, None])]
    broadcast_in_dim x16 -> x0, local copies, waits for them, and re-layouts: 1.96 us -> none  [the longest x7 0.89 us: combine_parts(): jnp.repeat(second_factor, head_dim, axis=1)]
    reduce_sum x3 -> x0, other arithmetic: 1.83 us -> none  [the longest x1 1.3 us: body(): used_total = jnp.sum(counts)]
  transfers between devices with their start and end apart: 2 -> 0, of which waited for: 1 -> 0; matrix products, arithmetic and copies ran while one was open for 1% -> 0% of each run, Pallas kernels for 0% -> 0%
where the time goes in v1:
time: 28.8 us; the launch traced here: 28.5 us
  Pallas kernels  27.2 us (94%)
  local copies, waits for them, and re-layouts  1.32 us (5%)
    pallas_call x1, Pallas kernels, body(): pl.pallas_call(functools.partial(mix_kernel, seqs, exponent_scale), out_s...  19.5 us
    pallas_call x1, Pallas kernels, body(): pl.pallas_call(functools.partial(attend_kernel, page_len, heads // kv_loc...  7.68 us
    unnamed x1, local copies, waits for them, and re-layouts  1.32 us

profile of v1, /device:TPU:0, one launch (start us, length us, event | category | flops | bytes accessed | tf_op | source)
XLA Modules:
  0.0 28.5 jit_solution(4783544622190805526)
XLA Ops:
  0.0 7.7 %shard_map.64 = (bf16[8,64,128]{2,1,0:T(8,128)(2,1)}, f32[8,2,128]{2,1,0:T(2,128)}) custom-call(s32[16]{0:T(128)} %lengths_ref.1, s32[256]{0:T(256)} %order_ref.1, bf16[16,32,128]{2,1,0:T(8,128)(2,1)} %query_ref.1, bf16[32,512,128]{2,1,0:T(8,128)(2,1)} %bitcast.2, bf16[32,512,128]{2,1,0:T(8,128)(2,1)} %bitcast.3), custom_call_target="tpu_custom_call" | custom-call | tf_op jit(solution)/shard_map/pallas_call | solution.py:326
  7.7 19.5 %shard_map.65 = bf16[8,1024]{1,0:T(8,128)(2,1)} custom-call(bf16[8,64,128]{2,1,0:T(8,128)(2,1)} %get-tuple-element.7.partial_ref, f32[8,2,128]{2,1,0:T(2,128)} %get-tuple-element.8.stats_ref, bf16[4096,1024]{1,0:T(8,128)(2,1)} %weight_hbm.1), custom_call_target="tpu_custom_call" | custom-call | tf_op jit(solution)/shard_map/pallas_call | solution.py:358
  27.2 1.3 %copy.8 = bf16[8,1024]{1,0:T(8,128)(2,1)} copy(bf16[8,1024]{1,0:T(8,128)(2,1)} %shard_map.65) | data formatting | bytes 32768

commit v2 on v1

v2 whole, which is shorter than its diff:
```python
import functools
import math

import jax
import jax.numpy as jnp
from jax import lax
from jax.experimental import pallas as pl
from jax.experimental.pallas import tpu as pltpu
from jax.sharding import PartitionSpec as P

MASKED = -1e30
FLOOR = -1e29
LANES = 128
UNROLL = 8
MESH = pl.DeviceIdType.MESH


def attend(
    page_len,
    group_size,
    chunk,
    step,
    exponent_scale,
    lengths_ref,
    order_ref,
    query_ref,
    key_hbm,
    value_hbm,
    out_ref,
    stats_ref,
    keys,
    values,
    scores,
    meta_vector,
    meta,
    block_top,
    run_top,
    run_total,
    run_out,
    by_head,
    key_sems,
    value_sems,
    meta_sem,
    when_loaded,
):
    pages, rows, head_dim = keys.shape
    seqs, heads, _ = query_ref.shape
    kv_local = rows // page_len
    shards, shard_rows, _ = out_ref.shape
    base = 2 * page_len

    def copies(hbm, buffer, sems):
        return [
            pltpu.make_async_copy(
                hbm.at[pl.ds(c * chunk, chunk)], buffer.at[pl.ds(c * chunk, chunk)], sems.at[c]
            )
            for c in range(pages // chunk)
        ]

    key_copies = copies(key_hbm, keys, key_sems)
    value_copies = copies(value_hbm, values, value_sems)
    for copy in key_copies + value_copies:
        copy.start()

    pool = order_ref.shape[0]
    order = order_ref[...].reshape(1, pool)
    rank = lax.broadcasted_iota(jnp.int32, (1, pool), 1)
    owner_row = jnp.zeros((1, pool), jnp.int32)
    limit_row = jnp.zeros((1, pool), jnp.int32)
    start = jnp.int32(0)
    for s in range(seqs):
        length = lengths_ref[s]
        reached = rank >= start
        owner_row = jnp.where(reached, s, owner_row)
        limit_row = jnp.where(reached, length + start * page_len, limit_row)
        start = start + lax.div(length + (page_len - 1), page_len)
    valid_row = jnp.clip(limit_row - rank * page_len, 0, page_len)
    packed = owner_row * base + valid_row
    local_page = lax.axis_index("seq") * pages + lax.broadcasted_iota(jnp.int32, (pages, pool), 0)
    is_page = order == local_page
    found = jnp.sum(jnp.where(is_page, packed, 0), axis=1, keepdims=True)
    found = jnp.clip(found, 0, seqs * base - 1)
    page_rank = jnp.sum(jnp.where(is_page, rank, 0), axis=1, keepdims=True)
    down = lax.broadcasted_iota(jnp.int32, (pages, LANES), 0)
    across = lax.broadcasted_iota(jnp.int32, (pages, LANES), 1)
    rank_across = jnp.sum(jnp.where(down == across, page_rank, 0), axis=0, keepdims=True)
    before = jnp.where((rank_across < page_rank) & (across < pages), 1, 0)
    place = jnp.sum(before, axis=1, keepdims=True)
    hit = place == across
    sorted_page = jnp.sum(jnp.where(hit, down, 0), axis=0, keepdims=True)
    sorted_packed = jnp.sum(jnp.where(hit, found, 0), axis=0, keepdims=True)
    sorted_page = jnp.clip(sorted_page, 0, pages - 1)
    sorted_packed = jnp.clip(sorted_packed, 0, seqs * base - 1)
    down = lax.broadcasted_iota(jnp.int32, (seqs, LANES), 0)
    across = lax.broadcasted_iota(jnp.int32, (seqs, LANES), 1)
    begun = (sorted_packed >= down * base) & (across < pages)
    ended = (sorted_packed >= (down + 1) * base) & (across < pages)
    begun = jnp.where(begun, 1, 0)
    ended = jnp.where(ended, 1, 0)
    held = jnp.sum(begun - ended, axis=1, keepdims=True)
    last = jnp.maximum(pages - 1 - jnp.sum(ended, axis=1, keepdims=True), 0)
    meta_vector[0:1] = sorted_page
    meta_vector[1:2] = sorted_packed
    meta_vector[8 : 8 + pages] = jnp.broadcast_to(found, (pages, LANES))
    meta_vector[8 + pages : 8 + pages + seqs] = jnp.where(across == 0, last, held)
    meta_copy = pltpu.make_async_copy(meta_vector, meta, meta_sem)
    meta_copy.start()

    column = lax.broadcasted_iota(jnp.int32, (heads, rows), 1)
    row_head = lax.broadcasted_iota(jnp.int32, (heads, rows), 0) // group_size
    column_limit = jnp.where(column % kv_local == row_head, column, rows)
    meta_copy.wait()

    for g in range(pages // step):
        for c in range(step // chunk):
            key_copies[g * (step // chunk) + c].wait()

        for i in range(step):
            p = g * step + i
            code = meta[8 + p, 0]
            count = lax.rem(code, base) * kv_local
            score = lax.dot_general(
                query_ref[lax.div(code, base)],
                keys[p],
                (((1,), (1,)), ((), ())),
                preferred_element_type=jnp.float32,
            )
            score = jnp.where(column_limit < count, score, MASKED)
            scores[p] = score
            block_max = jnp.maximum(jnp.max(score, axis=1, keepdims=True), FLOOR)
            block_top[p] = jnp.broadcast_to(block_max, (heads, LANES))

    def owner_at(i):
        return lax.div(meta[1, i], base)

    def kept_at(i):
        if i == 0:
            return jnp.float32(0.0)
        return jnp.where(owner_at(i) == owner_at(i - 1), 1.0, 0.0).astype(jnp.float32)

    running = jnp.full((heads, LANES), FLOOR, jnp.float32)
    for i in range(pages):
        kept = kept_at(i)
        floor = (1.0 - kept) * FLOOR
        running = jnp.maximum(running * kept + floor, block_top[meta[0, i]])
        run_top[i] = running

    for copy in value_copies:
        copy.wait()
    when_loaded()

    sum_so_far = jnp.zeros((heads, LANES), jnp.float32)
    out_so_far = jnp.zeros((heads, head_dim), jnp.float32)
    for i in range(pages):
        p = meta[0, i]
        top = run_top[meta[8 + pages + owner_at(i), 0]]
        highest = jnp.concatenate([top] * (rows // LANES), axis=1)
        weight = jnp.exp2((scores[p] - highest) * exponent_scale).astype(jnp.bfloat16)
        wide = weight.astype(jnp.float32)
        partial = wide[:, :LANES]
        for b in range(1, rows // LANES):
            partial = partial + wide[:, b * LANES : (b + 1) * LANES]
        kept = kept_at(i)
        product = jnp.dot(weight, values[p], preferred_element_type=jnp.float32)
        sum_so_far = sum_so_far * kept + partial
        out_so_far = out_so_far * kept + product
        run_total[i] = sum_so_far
        run_out[i] = out_so_far

    for s in range(seqs):
        where = pl.ds(s, heads, stride=seqs)
        at = meta[8 + pages + s, 0]
        some = meta[8 + pages + s, 1] > 0
        by_head[0, where, :] = jnp.where(some, run_out[at], 0.0)
        by_head[1, where, :] = jnp.where(some, run_top[at], FLOOR)
        total = jnp.sum(run_total[at], axis=1, keepdims=True)
        by_head[2, where, :] = jnp.broadcast_to(jnp.where(some, total, 0.0), (heads, LANES))
    out_ref[...] = by_head[0].reshape(shards, shard_rows, head_dim).astype(out_ref.dtype)
    diagonal = lax.broadcasted_iota(jnp.int32, (shard_rows, LANES), 0) == (
        lax.broadcasted_iota(jnp.int32, (shard_rows, LANES), 1)
    )
    for j in range(shards):
        for k in range(2):
            part = by_head[1 + k, j * shard_rows : (j + 1) * shard_rows, :]
            stats_ref[j, k : k + 1, :] = jnp.sum(
                jnp.where(diagonal, part, 0.0), axis=0, keepdims=True
            )


def partner(me, k, count):
    if count & (count - 1):
        return lax.rem(me + k, count)
    flipped = me + k
    bit = 1
    while bit < count:
        if k & bit:
            flipped = flipped - 2 * bit * lax.rem(lax.div(me, bit), 2)
        bit *= 2
    return flipped


def source_of(me, k, count):
    if count & (count - 1):
        return lax.rem(me + count - k, count)
    return partner(me, k, count)


def mix_kernel(
    page_len,
    group_size,
    chunk,
    step,
    exponent_scale,
    lengths_ref,
    order_ref,
    query_ref,
    key_hbm,
    value_hbm,
    weight_hbm,
    out_ref,
    keys,
    values,
    scores,
    meta_vector,
    meta,
    block_top,
    run_top,
    run_total,
    run_out,
    by_head,
    partial_ref,
    stats_ref,
    outs_in,
    stats_in,
    attended,
    weight,
    sums,
    sums_in,
    key_sems,
    value_sems,
    meta_sem,
    weight_sems,
    out_send,
    out_recv,
    stats_send,
    stats_recv,
    att_send,
    att_recv,
    sum_send,
    sum_recv,
):
    shards, shard_rows, head_dim = partial_ref.shape
    ways = sums.shape[0]
    far_first = range(shards - 1, 0, -1)
    seqs = query_ref.shape[0]
    me = lax.axis_index("seq")
    half = lax.axis_index("tensor")
    pieces = weight_sems.shape[0]
    depth = weight.shape[0] // pieces
    loads = []
    for c in range(pieces):
        part = pl.ds(c * depth, depth)
        loads.append(
            pltpu.make_async_copy(weight_hbm.at[part], weight.at[part], weight_sems.at[c])
        )

    barrier = pltpu.get_barrier_semaphore()
    for k in far_first:
        pl.semaphore_signal(
            barrier, inc=1, device_id={"seq": partner(me, k, shards)}, device_id_type=MESH
        )
    for k in range(1, ways):
        pl.semaphore_signal(
            barrier, inc=1, device_id={"tensor": lax.rem(half + k, ways)}, device_id_type=MESH
        )

    def start_loads():
        for load in loads:
            load.start()

    attend(
        page_len,
        group_size,
        chunk,
        step,
        exponent_scale,
        lengths_ref,
        order_ref,
        query_ref,
        key_hbm,
        value_hbm,
        partial_ref,
        stats_ref,
        keys,
        values,
        scores,
        meta_vector,
        meta,
        block_top,
        run_top,
        run_total,
        run_out,
        by_head,
        key_sems,
        value_sems,
        meta_sem,
        start_loads,
    )
    pl.semaphore_wait(barrier, shards + ways - 2)

    sends = []
    for k in far_first:
        peer = partner(me, k, shards)
        for source, target, send, recv in (
            (stats_ref, stats_in, stats_send, stats_recv),
            (partial_ref, outs_in, out_send, out_recv),
        ):
            copy = pltpu.make_async_remote_copy(
                src_ref=source.at[peer],
                dst_ref=target.at[k],
                send_sem=send.at[k],
                recv_sem=recv.at[k],
                device_id={"seq": peer},
                device_id_type=MESH,
            )
            copy.start()
            sends.append(copy)
    stats_in[0] = stats_ref[me]
    for copy in sends[0::2]:
        copy.wait_recv()
    tops = jnp.concatenate([stats_in[k, 0:1, :] for k in range(shards)], axis=0)
    totals = jnp.concatenate([stats_in[k, 1:2, :] for k in range(shards)], axis=0)
    factor = jnp.exp2((tops - jnp.max(tops, axis=0, keepdims=True)) * exponent_scale)
    denominator = jnp.sum(factor * totals, axis=0, keepdims=True)
    used = lax.broadcasted_iota(jnp.int32, (1, LANES), 1) < shard_rows
    share = factor / jnp.where(used, denominator, 1.0)
    diagonal = lax.broadcasted_iota(jnp.int32, (shard_rows, LANES), 0) == (
        lax.broadcasted_iota(jnp.int32, (shard_rows, LANES), 1)
    )

    def column(k):
        return jnp.sum(jnp.where(diagonal, share[k : k + 1, :], 0.0), axis=1, keepdims=True)

    columns = [column(k) for k in range(shards)]
    mine = columns[0] * partial_ref[me].astype(jnp.float32)
    for k in far_first:
        sends[2 * (shards - 1 - k) + 1].wait_recv()
        mine = mine + columns[k] * outs_in[k].astype(jnp.float32)
    attended[me] = mine.astype(jnp.bfloat16)

    gathers = []
    for k in far_first:
        copy = pltpu.make_async_remote_copy(
            src_ref=attended.at[me],
            dst_ref=attended.at[me],
            send_sem=att_send.at[k],
            recv_sem=att_recv.at[k],
            device_id={"seq": partner(me, k, shards)},
            device_id_type=MESH,
        )
        copy.start()
        gathers.append(copy)
    for load in loads:
        load.wait()

    whole_heads = shard_rows // seqs
    if shard_rows % seqs == 0:
        span = whole_heads * head_dim
        result = None
        for k in (0, *reversed(far_first)):
            source = source_of(me, k, shards)
            if k:
                pltpu.make_async_remote_copy(
                    src_ref=attended.at[source],
                    dst_ref=attended.at[source],
                    send_sem=att_send.at[k],
                    recv_sem=att_recv.at[k],
                    device_id={"seq": partner(me, k, shards)},
                    device_id_type=MESH,
                ).wait_recv()
            block = attended[source]
            left = jnp.concatenate(
                [block[h * seqs : (h + 1) * seqs] for h in range(whole_heads)], axis=1
            )
            rows = weight[pl.ds(pl.multiple_of(source * span, span), span), :]
            product = jnp.dot(left, rows, preferred_element_type=jnp.float32)
            result = product if result is None else result + product
    else:
        for k in far_first:
            gathers[shards - 1 - k].wait_recv()
        per_head = seqs // shard_rows
        result = None
        for h in range(shards // per_head):
            left = jnp.concatenate(
                [attended[h * per_head + i].astype(jnp.float32) for i in range(per_head)], axis=0
            ).astype(jnp.bfloat16)
            product = jnp.dot(
                left,
                weight[h * head_dim : (h + 1) * head_dim, :],
                preferred_element_type=jnp.float32,
            )
            result = product if result is None else result + product

    kept = seqs // ways
    for i in range(ways):
        sums[i] = result[i * kept : (i + 1) * kept]
    shares = []
    for k in range(1, ways):
        peer = lax.rem(half + k, ways)
        copy = pltpu.make_async_remote_copy(
            src_ref=sums.at[peer],
            dst_ref=sums_in.at[k - 1],
            send_sem=sum_send.at[k],
            recv_sem=sum_recv.at[k],
            device_id={"tensor": peer},
            device_id_type=MESH,
        )
        copy.start()
        shares.append(copy)
    mixed = sums[half]
    for k in range(1, ways):
        shares[k - 1].wait_recv()
        mixed = mixed + sums_in[k - 1]
    out_ref[...] = mixed.astype(out_ref.dtype)
    for copy in sends + gathers + shares:
        copy.wait_send()


def body(shards, ways, query, key_cache, value_cache, lengths, page_order, out_weight):
    pages, page_len, kv_local, head_dim = key_cache.shape
    seqs, heads, _ = query.shape
    rows = page_len * kv_local
    shard_rows = seqs * heads // shards
    depth, width = out_weight.shape
    kept = seqs // ways
    chunk = 4
    step = UNROLL
    exponent_scale = math.log2(math.e) / math.sqrt(head_dim)
    vmem = pl.BlockSpec(memory_space=pltpu.VMEM)
    smem = pl.BlockSpec(memory_space=pltpu.SMEM)
    hbm = pl.BlockSpec(memory_space=pl.ANY)
    f32, bf16 = jnp.float32, jnp.bfloat16
    dma = pltpu.SemaphoreType.DMA
    meta_rows = 8 + pages + seqs

    return pl.pallas_call(
        functools.partial(
            mix_kernel, page_len, heads // kv_local, chunk, step, exponent_scale
        ),
        out_shape=jax.ShapeDtypeStruct((kept, width), bf16),
        in_specs=[smem, vmem, vmem, hbm, hbm, hbm],
        out_specs=vmem,
        scratch_shapes=[
            pltpu.VMEM((pages, rows, head_dim), bf16),
            pltpu.VMEM((pages, rows, head_dim), bf16),
            pltpu.VMEM((pages, heads, rows), f32),
            pltpu.VMEM((meta_rows, LANES), jnp.int32),
            pltpu.SMEM((meta_rows, LANES), jnp.int32),
            pltpu.VMEM((pages, heads, LANES), f32),
            pltpu.VMEM((pages, heads, LANES), f32),
            pltpu.VMEM((pages, heads, LANES), f32),
            pltpu.VMEM((pages, heads, head_dim), f32),
            pltpu.VMEM((3, seqs * heads, LANES), f32),
            pltpu.VMEM((shards, shard_rows, head_dim), bf16),
            pltpu.VMEM((shards, 2, LANES), f32),
            pltpu.VMEM((shards, shard_rows, head_dim), bf16),
            pltpu.VMEM((shards, 2, LANES), f32),
            pltpu.VMEM((shards, shard_rows, head_dim), bf16),
            pltpu.VMEM((depth, width), bf16),
            pltpu.VMEM((ways, kept, width), f32),
            pltpu.VMEM((max(ways - 1, 1), kept, width), f32),
            dma((pages // chunk,)),
            dma((pages // chunk,)),
            dma,
            dma((8,)),
            dma((shards,)),
            dma((shards,)),
            dma((shards,)),
            dma((shards,)),
            dma((shards,)),
            dma((shards,)),
            dma((ways,)),
            dma((ways,)),
        ],
        compiler_params=pltpu.CompilerParams(collective_id=0, has_side_effects=True),
    )(
        lengths,
        page_order,
        query,
        key_cache.reshape(pages, rows, head_dim),
        value_cache.reshape(pages, rows, head_dim),
        out_weight,
    )


def solution(mesh):
    in_specs = (
        P("group", "tensor", None),
        P(("group", "seq"), None, "tensor", None),
        P(("group", "seq"), None, "tensor", None),
        P("group"),
        P("group"),
        P("tensor", "seq"),
    )
    out_specs = P(("group", "tensor"), "seq")
    step = functools.partial(body, mesh.shape["seq"], mesh.shape["tensor"])
    return jax.shard_map(step, mesh=mesh, in_specs=in_specs, out_specs=out_specs, check_vma=False)
```

time: 28.8 us -> 23 us (0.80)
  Pallas kernels: 27.2 us -> 21.5 us
    pallas_call x2 -> x1, Pallas kernels: 27.2 us -> 21.5 us  [body(): pl.pallas_call(functools.partial(mix_kernel, page_len, heads // kv_local,...]
where the time goes in v2:
time: 23 us; the launch traced here: 22.8 us
  Pallas kernels  21.5 us (93%)
  local copies, waits for them, and re-layouts  1.32 us (6%)
    pallas_call x1, Pallas kernels, body(): pl.pallas_call(functools.partial(mix_kernel, page_len, heads // kv_local,...  21.5 us
    unnamed x1, local copies, waits for them, and re-layouts  1.32 us

profile of v2, /device:TPU:0, one launch (start us, length us, event | category | flops | bytes accessed | tf_op | source)
XLA Modules:
  0.0 22.8 jit_solution(13157816007077824567)
XLA Ops:
  0.0 21.5 %shard_map.64 = bf16[8,1024]{1,0:T(8,128)(2,1)} custom-call(s32[16]{0:T(128)} %lengths_ref.1, s32[256]{0:T(256)} %order_ref.1, bf16[16,32,128]{2,1,0:T(8,128)(2,1)} %query_ref.1, bf16[32,512,128]{2,1,0:T(8,128)(2,1)} %bitcast.2, bf16[32,512,128]{2,1,0:T(8,128)(2,1)} %bitcast.3, bf16[4096,1024]{1,0:T(8,128)(2,1)} %weight_hbm.1), custom_call_target="tpu_custom_call" | custom-call | tf_op jit(solution)/shard_map/pallas_call | solution.py:446
  21.5 1.3 %copy.8 = bf16[8,1024]{1,0:T(8,128)(2,1)} copy(bf16[8,1024]{1,0:T(8,128)(2,1)} %shard_map.64) | data formatting | bytes 32768

commit v3 on v2

--- a/solution.py
+++ b/solution.py
@@ -12,6 +12,7 @@
 FLOOR = -1e29
 LANES = 128
 UNROLL = 8
+HALVES = 2
 MESH = pl.DeviceIdType.MESH
 
 
@@ -42,6 +43,8 @@
     value_sems,
     meta_sem,
     when_loaded,
+    order_copy,
+    query_copy,
 ):
     pages, rows, head_dim = keys.shape
     seqs, heads, _ = query_ref.shape
@@ -62,6 +65,7 @@
     for copy in key_copies + value_copies:
         copy.start()
 
+    order_copy.wait()
     pool = order_ref.shape[0]
     order = order_ref[...].reshape(1, pool)
     rank = lax.broadcasted_iota(jnp.int32, (1, pool), 1)
@@ -110,6 +114,7 @@
     row_head = lax.broadcasted_iota(jnp.int32, (heads, rows), 0) // group_size
     column_limit = jnp.where(column % kv_local == row_head, column, rows)
     meta_copy.wait()
+    query_copy.wait()
 
     for g in range(pages // step):
         for c in range(step // chunk):
@@ -212,12 +217,14 @@
     step,
     exponent_scale,
     lengths_ref,
-    order_ref,
-    query_ref,
+    order_hbm,
+    query_hbm,
     key_hbm,
     value_hbm,
     weight_hbm,
     out_ref,
+    order_ref,
+    query_ref,
     keys,
     values,
     scores,
@@ -239,6 +246,7 @@
     key_sems,
     value_sems,
     meta_sem,
+    input_sems,
     weight_sems,
     out_send,
     out_recv,
@@ -255,6 +263,10 @@
     seqs = query_ref.shape[0]
     me = lax.axis_index("seq")
     half = lax.axis_index("tensor")
+    order_copy = pltpu.make_async_copy(order_hbm, order_ref, input_sems.at[0])
+    query_copy = pltpu.make_async_copy(query_hbm, query_ref, input_sems.at[1])
+    order_copy.start()
+    query_copy.start()
     pieces = weight_sems.shape[0]
     depth = weight.shape[0] // pieces
     loads = []
@@ -305,61 +317,71 @@
         value_sems,
         meta_sem,
         start_loads,
+        order_copy,
+        query_copy,
     )
     pl.semaphore_wait(barrier, shards + ways - 2)
 
-    sends = []
+    cuts = HALVES if shard_rows % (16 * HALVES) == 0 else 1
+    span_rows = shard_rows // cuts
+    parts = [pl.ds(h * span_rows, span_rows) for h in range(cuts)]
+    stats_copies, out_copies, gathers = {}, {}, {}
     for k in far_first:
         peer = partner(me, k, shards)
-        for source, target, send, recv in (
-            (stats_ref, stats_in, stats_send, stats_recv),
-            (partial_ref, outs_in, out_send, out_recv),
-        ):
-            copy = pltpu.make_async_remote_copy(
-                src_ref=source.at[peer],
-                dst_ref=target.at[k],
-                send_sem=send.at[k],
-                recv_sem=recv.at[k],
+        stats_copies[k] = pltpu.make_async_remote_copy(
+            src_ref=stats_ref.at[peer],
+            dst_ref=stats_in.at[k],
+            send_sem=stats_send.at[k],
+            recv_sem=stats_recv.at[k],
+            device_id={"seq": peer},
+            device_id_type=MESH,
+        )
+        stats_copies[k].start()
+    for h in range(cuts):
+        for k in far_first:
+            peer = partner(me, k, shards)
+            out_copies[h, k] = pltpu.make_async_remote_copy(
+                src_ref=partial_ref.at[peer, parts[h]],
+                dst_ref=outs_in.at[k, parts[h]],
+                send_sem=out_send.at[h * shards + k],
+                recv_sem=out_recv.at[h * shards + k],
                 device_id={"seq": peer},
                 device_id_type=MESH,
             )
-            copy.start()
-            sends.append(copy)
+            out_copies[h, k].start()
     stats_in[0] = stats_ref[me]
-    for copy in sends[0::2]:
-        copy.wait_recv()
+    for k in far_first:
+        stats_copies[k].wait_recv()
     tops = jnp.concatenate([stats_in[k, 0:1, :] for k in range(shards)], axis=0)
     totals = jnp.concatenate([stats_in[k, 1:2, :] for k in range(shards)], axis=0)
     factor = jnp.exp2((tops - jnp.max(tops, axis=0, keepdims=True)) * exponent_scale)
     denominator = jnp.sum(factor * totals, axis=0, keepdims=True)
     used = lax.broadcasted_iota(jnp.int32, (1, LANES), 1) < shard_rows
     share = factor / jnp.where(used, denominator, 1.0)
-    diagonal = lax.broadcasted_iota(jnp.int32, (shard_rows, LANES), 0) == (
-        lax.broadcasted_iota(jnp.int32, (shard_rows, LANES), 1)
-    )
-
-    def column(k):
+
+    def column(h, k):
+        diagonal = lax.broadcasted_iota(jnp.int32, (span_rows, LANES), 0) + h * span_rows == (
+            lax.broadcasted_iota(jnp.int32, (span_rows, LANES), 1)
+        )
         return jnp.sum(jnp.where(diagonal, share[k : k + 1, :], 0.0), axis=1, keepdims=True)
 
-    columns = [column(k) for k in range(shards)]
-    mine = columns[0] * partial_ref[me].astype(jnp.float32)
-    for k in far_first:
-        sends[2 * (shards - 1 - k) + 1].wait_recv()
-        mine = mine + columns[k] * outs_in[k].astype(jnp.float32)
-    attended[me] = mine.astype(jnp.bfloat16)
-
-    gathers = []
-    for k in far_first:
-        copy = pltpu.make_async_remote_copy(
-            src_ref=attended.at[me],
-            dst_ref=attended.at[me],
-            send_sem=att_send.at[k],
-            recv_sem=att_recv.at[k],
-            device_id={"seq": partner(me, k, shards)},
-            device_id_type=MESH,
-        )
-        copy.start()
-        gathers.append(copy)
+    columns = {(h, k): column(h, k) for h in range(cuts) for k in range(shards)}
+    for h in range(cuts):
+        mine = columns[h, 0] * partial_ref[me, parts[h], :].astype(jnp.float32)
+        for k in reversed(far_first):
+            out_copies[h, k].wait_recv()
+            mine = mine + columns[h, k] * outs_in[k, parts[h], :].astype(jnp.float32)
+        attended[me, parts[h], :] = mine.astype(jnp.bfloat16)
+        for k in far_first:
+            gathers[h, k] = pltpu.make_async_remote_copy(
+                src_ref=attended.at[me, parts[h]],
+                dst_ref=attended.at[me, parts[h]],
+                send_sem=att_send.at[h * shards + k],
+                recv_sem=att_recv.at[h * shards + k],
+                device_id={"seq": partner(me, k, shards)},
+                device_id_type=MESH,
+            )
+            gathers[h, k].start()
     for load in loads:
         load.wait()
 
@@ -369,12 +391,12 @@
         result = None
         for k in (0, *reversed(far_first)):
             source = source_of(me, k, shards)
-            if k:
+            for h in range(cuts if k else 0):
                 pltpu.make_async_remote_copy(
-                    src_ref=attended.at[source],
-                    dst_ref=attended.at[source],
-                    send_sem=att_send.at[k],
-                    recv_sem=att_recv.at[k],
+                    src_ref=attended.at[source, parts[h]],
+                    dst_ref=attended.at[source, parts[h]],
+                    send_sem=att_send.at[h * shards + k],
+                    recv_sem=att_recv.at[h * shards + k],
                     device_id={"seq": partner(me, k, shards)},
                     device_id_type=MESH,
                 ).wait_recv()
@@ -387,7 +409,7 @@
             result = product if result is None else result + product
     else:
         for k in far_first:
-            gathers[shards - 1 - k].wait_recv()
+            gathers[0, k].wait_recv()
         per_head = seqs // shard_rows
         result = None
         for h in range(shards // per_head):
@@ -422,7 +444,8 @@
         shares[k - 1].wait_recv()
         mixed = mixed + sums_in[k - 1]
     out_ref[...] = mixed.astype(out_ref.dtype)
-    for copy in sends + gathers + shares:
+    sent = [*stats_copies.values(), *out_copies.values(), *gathers.values()]
+    for copy in sent + shares:
         copy.wait_send()
 
 
@@ -448,9 +471,11 @@
             mix_kernel, page_len, heads // kv_local, chunk, step, exponent_scale
         ),
         out_shape=jax.ShapeDtypeStruct((kept, width), bf16),
-        in_specs=[smem, vmem, vmem, hbm, hbm, hbm],
+        in_specs=[smem, hbm, hbm, hbm, hbm, hbm],
         out_specs=vmem,
         scratch_shapes=[
+            pltpu.VMEM(page_order.shape, jnp.int32),
+            pltpu.VMEM(query.shape, bf16),
             pltpu.VMEM((pages, rows, head_dim), bf16),
             pltpu.VMEM((pages, rows, head_dim), bf16),
             pltpu.VMEM((pages, heads, rows), f32),
@@ -472,13 +497,14 @@
             dma((pages // chunk,)),
             dma((pages // chunk,)),
             dma,
+            dma((2,)),
             dma((8,)),
+            dma((HALVES * shards,)),
+            dma((HALVES * shards,)),
             dma((shards,)),
             dma((shards,)),
-            dma((shards,)),
-            dma((shards,)),
-            dma((shards,)),
-            dma((shards,)),
+            dma((HALVES * shards,)),
+            dma((HALVES * shards,)),
             dma((ways,)),
             dma((ways,)),
         ],

time: 23 us -> 22.9 us (level)
  no operation moved by 1% of the time
where the time goes in v3:
time: 22.9 us; the launch traced here: 22.6 us
  Pallas kernels  21.3 us (93%)
  local copies, waits for them, and re-layouts  1.32 us (6%)
    pallas_call x1, Pallas kernels, body(): pl.pallas_call(functools.partial(mix_kernel, page_len, heads // kv_local,...  21.3 us
    unnamed x1, local copies, waits for them, and re-layouts  1.32 us

profile of v3, /device:TPU:0, one launch (start us, length us, event | category | flops | bytes accessed | tf_op | source)
XLA Modules:
  0.0 22.6 jit_solution(3894346926330387410)
XLA Ops:
  0.0 21.3 %shard_map.64 = bf16[8,1024]{1,0:T(8,128)(2,1)} custom-call(s32[16]{0:T(128)} %lengths_ref.1, s32[256]{0:T(256)} %order_hbm.1, bf16[16,32,128]{2,1,0:T(8,128)(2,1)} %query_hbm.1, bf16[32,512,128]{2,1,0:T(8,128)(2,1)} %bitcast.2, bf16[32,512,128]{2,1,0:T(8,128)(2,1)} %bitcast.3, bf16[4096,1024]{1,0:T(8,128)(2,1)} %weight_hbm.1), custom_call_target="tpu_custom_call" | custom-call | tf_op jit(solution)/shard_map/pallas_call | solution.py:469
  21.3 1.3 %copy.8 = bf16[8,1024]{1,0:T(8,128)(2,1)} copy(bf16[8,1024]{1,0:T(8,128)(2,1)} %shard_map.64) | data formatting | bytes 32768
